TPU v7x, 32 devices: a whole 2x2x4 slice. The times are simulated.
32 devices in a mesh: graph: 16 (over z, y, core), chan: 2 (over x).
Axes of the slice: x: 2, y: 2, z: 4, core: 2. Of those that a mesh axis runs over, the one named last changes fastest.
Arguments:
- embed: bfloat16 [25, 512, 2048], P(None, 'chan', 'graph'), may hold values from -200 to 200
- gain: float32 [5, 512], P(None, 'chan'), may hold values from 0.25 to 1.75
- w_zero: bfloat16 [5, 512, 2560], P(None, 'chan'), may hold values from -0.125 to 0.125
- w_one: bfloat16 [2, 4, 512, 2048], P(None, None, 'chan'), may hold values from -0.125 to 0.125
- w_two: bfloat16 [2, 3, 512, 1536], P(None, None, 'chan'), may hold values from -0.15625 to 0.15625
- rot_table: float32 [19, 25, 256], replicated, may hold values from -1 to 1, as said below
- face_atoms: int32 [512], P('graph'), may hold values from 0 to 127, as said below
- edge_source: int32 [2048], P('graph'), may hold values from 0 to 159
- edge_target: int32 [2048], P('graph'), may hold values from 0 to 127
- rot_index: int32 [2048], P('graph'), may hold values from 0 to 255
- edge_weight: float32 [2048], P('graph'), may hold values from 0.2 to 1
- cotangent: bfloat16 [25, 512, 2048], P(None, 'chan', 'graph'), may hold values from -1.5 to 1.5
Outputs:
- update: bfloat16 [25, 512, 2048], P(None, 'chan', 'graph')
- grad_embed: bfloat16 [25, 512, 2048], P(None, 'chan', 'graph')
- grad_zero: float32 [5, 512, 2560], P(None, 'chan', 'graph')
- grad_one: float32 [2, 4, 512, 2048], P(None, None, 'chan', 'graph')
- grad_two: float32 [2, 3, 512, 1536], P(None, None, 'chan', 'graph')
Inputs may be any that keep to these rules, and one draw needn't show every extreme that they name: `rot_table`: for every rotation, frame row (m, l) is nonzero only on the 2l + 1 coefficients of degree l, where it is row l + m of an orthogonal (2l + 1)-square matrix shared by the rows of that degree; the degree-0 entry is 1. `face_atoms`: block b holds 32 distinct atom indices counted from the first atom of block b: the first 16 lie at the face toward block b - 1, the last 16 at the face toward block b + 1. `edge_source`: read as in the step that defines src. `edge_target`: counted from the first atom of the edge's block.
All inputs are finite; a program needn't handle non-finite values.
Results may differ from a plain program's by a relative error of at most 0.0062.
Values may be sent and summed in bfloat16 or wider, within the bound.
A program may use at most 192 MiB of HBM per device.

v0:
```python
import functools

import jax
import jax.numpy as jnp
from jax import lax
from jax.experimental import pallas as pl
from jax.experimental.pallas import tpu as pltpu
from jax.sharding import PartitionSpec as P


EPSILON = 1e-06
HIGHEST = lax.Precision.HIGHEST
FRAME = (
    (0, 0),
    (1, 0),
    (2, 0),
    (3, 0),
    (4, 0),
    (1, 1),
    (2, 1),
    (3, 1),
    (4, 1),
    (1, -1),
    (2, -1),
    (3, -1),
    (4, -1),
    (2, 2),
    (3, 2),
    (4, 2),
    (2, -2),
    (3, -2),
    (4, -2),
)


def gain_rows(gain):
    pieces = [
        jnp.broadcast_to(gain[degree : degree + 1], (2 * degree + 1, gain.shape[1]))
        for degree in range(5)
    ]
    return jnp.concatenate(pieces, axis=0)


def product(left, right):
    return jnp.dot(left, right, preferred_element_type=jnp.float32)


def across(left, right):
    return lax.dot_general(
        left, right, (((0,), (0,)), ((), ())), preferred_element_type=jnp.float32
    )


def contract(left, right):
    return lax.dot_general(left, right, (((2,), (1,)), ((), ())), preferred_element_type=jnp.float32)


def frames_kernel(*refs):
    pairs, (rotations, scale, out) = refs[:-3], refs[-3:]
    count, width = pairs[0].shape[0], pairs[0].shape[1]
    total = None
    for values, picks in zip(pairs[0::2], pairs[1::2]):
        part = product(values[...].reshape(count * width, values.shape[2]), picks[...])
        total = part if total is None else total + part
    total = total.reshape(count, width, total.shape[1])
    for row, (degree, _) in enumerate(FRAME):
        first = degree * degree
        entry = row * count + first
        line = rotations[entry : entry + 1, :] * total[first]
        for step in range(1, 2 * degree + 1):
            entry = row * count + first + step
            line = line + rotations[entry : entry + 1, :] * total[first + step]
        out[row] = (line * scale[...]).astype(out.dtype)


def to_frames(pairs, rotations, scale):
    count, local = pairs[0][0].shape[0], pairs[0][0].shape[1]
    edges = scale.shape[1]
    block = min(64, local)
    operands, specs = [], []
    for values, picks in pairs:
        operands += [values, picks]
        specs.append(pl.BlockSpec((count, block, values.shape[2]), lambda i: (0, i, 0)))
        specs.append(pl.BlockSpec(picks.shape, lambda i: (0, 0)))
    for whole in (rotations, scale):
        operands.append(whole)
        specs.append(pl.BlockSpec(whole.shape, lambda i: (0, 0)))
    return pl.pallas_call(
        frames_kernel,
        grid=(local // block,),
        in_specs=specs,
        out_specs=pl.BlockSpec((len(FRAME), block, edges), lambda i: (0, i, 0)),
        out_shape=jax.ShapeDtypeStruct((len(FRAME), local, edges), jnp.bfloat16),
        compiler_params=pltpu.CompilerParams(dimension_semantics=("arbitrary",)),
    )(*operands)


def atoms_kernel(count, values, rotations, scale, *refs):
    picks, outs, held = refs[: len(refs) // 2], refs[len(refs) // 2 : -1], refs[-1]
    width, edges = values.shape[1], values.shape[2]
    for degree in range(5):
        members = [row for row, pair in enumerate(FRAME) if pair[0] == degree]
        lines = [values[row].astype(jnp.float32) * scale[...] for row in members]
        for column in range(degree * degree, (degree + 1) * (degree + 1)):
            total = None
            for row, line in zip(members, lines):
                entry = row * count + column
                term = rotations[entry : entry + 1, :] * line
                total = term if total is None else total + term
            held[column] = total.astype(held.dtype)
    flat = held[...].reshape(count * width, edges)
    for pick, out in zip(picks, outs):
        out[...] = product(flat, pick[...]).reshape(out.shape).astype(out.dtype)


def to_atoms(values, rotations, scale, picks, kinds):
    rows, local, edges = values.shape
    count = rotations.shape[0] // rows
    block = min(64, local)
    whole = lambda i: (0, 0)
    return pl.pallas_call(
        functools.partial(atoms_kernel, count),
        grid=(local // block,),
        in_specs=[
            pl.BlockSpec((rows, block, edges), lambda i: (0, i, 0)),
            pl.BlockSpec(rotations.shape, whole),
            pl.BlockSpec(scale.shape, whole),
        ]
        + [pl.BlockSpec(pick.shape, whole) for pick in picks],
        out_specs=[
            pl.BlockSpec((count, block, pick.shape[1]), lambda i: (0, i, 0)) for pick in picks
        ],
        out_shape=[
            jax.ShapeDtypeStruct((count, local, pick.shape[1]), kind)
            for pick, kind in zip(picks, kinds)
        ],
        scratch_shapes=[pltpu.VMEM((count, block, edges), jnp.bfloat16)],
        compiler_params=pltpu.CompilerParams(dimension_semantics=("arbitrary",)),
    )(values, rotations, scale, *picks)


def swap(block, bit):
    count = lax.axis_size("graph")
    return lax.ppermute(block, "graph", [(i, i ^ bit) for i in range(count)])


def from_beside(faces, width):
    count = lax.axis_size("graph")
    forward = [(i, (i + 1) % count) for i in range(count)]
    backward = [(target, source) for source, target in forward]
    low = lax.ppermute(faces[:, :, width:], "graph", forward)
    high = lax.ppermute(faces[:, :, :width], "graph", backward)
    return jnp.concatenate([low, high], axis=2)


def hot_rows(size, codes):
    return (jnp.arange(size, dtype=jnp.int32)[:, None] == codes[None, :]).astype(jnp.bfloat16)


def hot_columns(codes, size):
    return (codes[:, None] == jnp.arange(size, dtype=jnp.int32)[None, :]).astype(jnp.bfloat16)


def beside(plus, minus, axis=-1):
    return jnp.concatenate([plus, minus], axis=axis)


def mix_forward(weights, frame):
    w_zero, w_one, w_two = weights
    edges = frame.shape[2]
    local = w_zero.shape[1]
    mixed = [
        product(w_zero.reshape(-1, w_zero.shape[2]), frame[:5].reshape(-1, edges)).reshape(
            5, local, edges
        )
    ]
    for weight, first, blocks in ((w_one, 5, 4), (w_two, 13, 3)):
        plus = frame[first : first + blocks].reshape(-1, edges)
        minus = frame[first + blocks : first + 2 * blocks].reshape(-1, edges)
        both = product(weight.reshape(-1, weight.shape[-1]), beside(plus, minus))
        both = both.reshape(2, blocks, local, 2 * edges)
        mixed.append(both[0, :, :, :edges] - both[1, :, :, edges:])
        mixed.append(both[0, :, :, edges:] + both[1, :, :, :edges])
    return jnp.concatenate(mixed, axis=0)


def mix_back(weights, grads, shares):
    w_zero, w_one, w_two = weights
    edges = grads.shape[2]

    def shared(block, blocks):
        shaped = block.reshape(blocks, shares, -1, edges).astype(jnp.bfloat16)
        return jnp.transpose(shaped, (1, 0, 2, 3))

    back = [
        shared(across(w_zero.reshape(-1, w_zero.shape[2]), grads[:5].reshape(-1, edges)), 5)
    ]
    for weight, first, blocks in ((w_one, 5, 4), (w_two, 13, 3)):
        plus = grads[first : first + blocks].reshape(-1, edges)
        minus = grads[first + blocks : first + 2 * blocks].reshape(-1, edges)
        sides = jnp.concatenate([beside(plus, minus), beside(minus, -plus)], axis=0)
        both = across(weight.reshape(-1, weight.shape[-1]), sides)
        back.append(shared(both[:, :edges], blocks))
        back.append(shared(both[:, edges:], blocks))
    return jnp.concatenate(back, axis=1)


def column_frames(frame):
    count = lax.axis_size("graph")
    near = 4
    far = count // near
    edges = frame.shape[2]
    cuts = ((0, 5), (5, 4), (9, 4), (13, 3), (16, 3))
    parts = [
        frame[first : first + blocks].reshape(far, near, -1, edges) for first, blocks in cuts
    ]
    widths = [part.shape[2] for part in parts]
    packed = jnp.concatenate(parts, axis=2)
    mine = lax.axis_index("graph") % near
    frames = []
    for bit in (0, 2, 1, 3):
        target = mine ^ bit
        chunk = lax.dynamic_index_in_dim(packed, target, axis=1, keepdims=False)
        frames.append(swap(chunk, bit) if bit else chunk)
    return frames, widths


def weight_grads(frames, widths, grads_all, local):
    count = lax.axis_size("graph")
    near = 4
    far = count // near
    edges = frames[0].shape[2]
    starts = [sum(widths[:i]) for i in range(5)]
    groups = [[z * near + q for z in range(far)] for q in range(near)]

    def settle(partial):
        return lax.psum_scatter(
            partial.astype(jnp.bfloat16),
            "graph",
            scatter_dimension=0,
            axis_index_groups=groups,
            tiled=False,
        ).astype(jnp.float32)

    def settle_direct(partial):
        partial = partial.astype(jnp.bfloat16)
        place = lax.axis_index("graph") // near
        total = lax.dynamic_index_in_dim(partial, place, axis=0, keepdims=False)
        total = total.astype(jnp.float32)
        for step in range(1, far):
            chunk = lax.dynamic_index_in_dim(partial, (place + step) % far, axis=0, keepdims=False)
            shift = [(i, (i + step * near) % count) for i in range(count)]
            total = total + lax.ppermute(chunk, "graph", shift).astype(jnp.float32)
        return total

    def columns(index):
        return [chunk[:, starts[index] : starts[index] + widths[index]] for chunk in frames]

    left = jnp.concatenate(columns(0), axis=2)
    right = jnp.concatenate([g[:5].reshape(-1, edges) for g in grads_all], axis=1)
    done = settle_direct(contract(left, right))
    results = [jnp.transpose(done).reshape(5, local, widths[0])]
    for index, first, blocks in ((1, 5, 4), (3, 13, 3)):
        plus, minus = columns(index), columns(index + 1)
        real_part = jnp.concatenate([x for pair in zip(plus, minus) for x in pair], axis=2)
        imag_part = jnp.concatenate([x for pair in zip(minus, plus) for x in (-pair[0], pair[1])], axis=2)
        left = jnp.concatenate([real_part, imag_part], axis=1)
        right = jnp.concatenate(
            [
                g[start : start + blocks].reshape(-1, edges)
                for g in grads_all
                for start in (first, first + blocks)
            ],
            axis=1,
        )
        done = settle(contract(left, right))
        done = done.reshape(2, widths[index], blocks * local)
        results.append(jnp.transpose(done, (0, 2, 1)).reshape(2, blocks, local, widths[index]))
    return results


NEAR = 4
PARTS = ((5, 1), (4, 2), (3, 2))
FIRSTS = (0, 5, 13)


def lanes(start, size):
    return pl.ds(pl.multiple_of(start, 128), size)


def turned(left, right):
    return lax.dot_general(
        left, right, (((1,), (1,)), ((), ())), preferred_element_type=jnp.float32
    )


def hot(size, codes, first=0):
    places = lax.broadcasted_iota(jnp.int32, (size, codes.shape[1]), 0) + first
    return (places == codes).astype(jnp.bfloat16)


class Links:
    def __init__(self, sends, recvs):
        self.sends, self.recvs, self.count, self.started = sends, recvs, 0, []

    def start(self, source, target, device):
        index = self.count
        self.count += 1
        copy = pltpu.make_async_remote_copy(
            src_ref=source,
            dst_ref=target,
            send_sem=self.sends.at[index],
            recv_sem=self.recvs.at[index],
            device_id=device,
            device_id_type=pl.DeviceIdType.MESH,
        )
        copy.start()
        self.started.append(copy)
        return copy

    def settle(self, copy):
        copy.wait_send()
        self.started = [one for one in self.started if one is not copy]

    def finish(self):
        for copy in self.started:
            copy.wait_send()


def layer_kernel(shares, count, *refs):
    (embed, cotangent, gain, w_zero, w_one, w_two, table) = refs[:7]
    (face_row, source_row, target_row, which_row, weight_row) = refs[7:12]
    (update, grad_embed, out_zero, out_one, out_two) = refs[12:17]
    weights = refs[17:20]
    frames = refs[20:23]
    grads = refs[23:26]
    doubled = (None,) + tuple(refs[26:28])
    nears = refs[28:31]
    back_out, back_in = refs[31:34], refs[34:37]
    kept, leaving, arriving, final = refs[37:40], refs[40:43], refs[43:46], refs[46:49]
    (work, back, arrow, values, normed, rot, gains) = refs[49:56]
    (face_out, face_in, ends_out, ends_in) = refs[56:60]
    (square_out, square_in, tally_out, tally_in) = refs[60:64]
    sends, recvs, local_sems = refs[64:67]
    outs = (out_zero, out_one, out_two)
    f32, bf16 = jnp.float32, jnp.bfloat16
    terms, width, atoms = values.shape
    edges = source_row.shape[1]
    halo = face_row.shape[1] // 2
    channels = width * shares
    me = lax.axis_index("graph")
    share = lax.axis_index("chan")
    low, side, pair, far = me % 2, (me // 2) % 2, (me // 4) % 2, (me // 8) % 2
    slot = pair * 2 + low

    def flip(bit):
        digits = {1: low, 2: side, 4: pair, 8: far}
        place = me
        for one in (1, 2, 4, 8):
            if bit & one:
                place = place + one - 2 * one * digits[one]
        return (place, share)

    after, before = (lax.rem(me + 1, count), share), (lax.rem(me + count - 1, count), share)
    peers = [lax.rem(share + step, shares) for step in range(1, shares)]
    copies = []

    def bring(origin, target):
        copy = pltpu.make_async_copy(origin, target, local_sems.at[len(copies)])
        copy.start()
        copies.append(copy)
        return copy

    load_embed = bring(embed, values)
    load_cotangent = bring(cotangent, arrow)
    order = (1, 0, 2)
    loads = {at: bring((w_zero, w_one, w_two)[at], weights[at]) for at in order}

    barrier = pltpu.get_barrier_semaphore()
    others = [flip(bit) for bit in (1, 2, 4, 5, 8)] + [after, before]
    others += [(me, peer) for peer in peers]
    for other in others:
        pl.semaphore_signal(
            barrier, inc=1, device_id=other, device_id_type=pl.DeviceIdType.MESH
        )
    links = Links(sends, recvs)

    which = hot(table.shape[2], which_row[...]).astype(f32)

    def turn(row, unused):
        rot[row] = jnp.dot(
            table[row], which, precision=HIGHEST, preferred_element_type=f32
        )
        return unused

    lax.fori_loop(0, len(FRAME), turn, 0)
    degrees = lax.broadcasted_iota(jnp.int32, (5, atoms), 0)
    for degree in range(5):
        gains[degree] = lax.dot_general(
            gain[...],
            (degrees == degree).astype(f32),
            (((0,), (0,)), ((), ())),
            precision=HIGHEST,
            preferred_element_type=f32,
        )
    to_target = hot(atoms, target_row[...])
    to_source = hot(atoms, source_row[...])
    to_halo = hot(2 * halo, source_row[...], atoms)
    faces = hot(atoms, face_row[...])
    square = lax.broadcasted_iota(jnp.int32, (2 * halo, 2 * halo), 0)
    unit = (square == lax.broadcasted_iota(jnp.int32, square.shape, 1)).astype(bf16)
    to_face = turned(unit, faces).astype(bf16)
    scale = weight_row[...]

    load_embed.wait()

    def squared(term, total):
        value = values[term].astype(f32)
        return total + value * value

    total = lax.fori_loop(0, terms, squared, jnp.zeros((width, atoms), f32))
    own_squares = jnp.sum(total, axis=0, keepdims=True)
    square_out[...] = jnp.broadcast_to(own_squares, square_out.shape)
    pl.semaphore_wait(barrier, len(others))
    summed = [
        links.start(square_out, square_in.at[index], (me, peer))
        for index, peer in enumerate(peers)
    ]

    def spread(values_ref, picks):
        def one(term, unused):
            work[term] = product(values_ref[term], picks)
            return unused

        lax.fori_loop(0, terms, one, 0)

    tall = min(32, width)

    def rotate(at, put):
        first, (blocks, parts) = FIRSTS[at], PARTS[at]

        def one(step, unused):
            rows = pl.ds(pl.multiple_of(step * tall, tall), tall)
            for degree in range(5):
                base = degree * degree
                members = [
                    row
                    for row in range(first, first + blocks * parts)
                    if FRAME[row][0] == degree
                ]
                if not members:
                    continue
                lines = [work[base + index, rows, :] for index in range(2 * degree + 1)]
                for row in members:
                    line = None
                    for index, entry in enumerate(lines):
                        term = rot[row, base + index : base + index + 1, :] * entry
                        line = term if line is None else line + term
                    part, block = divmod(row - first, blocks)
                    put(block, part, step * tall, line)
            return unused

        lax.fori_loop(0, width // tall, one, 0)

    load_cotangent.wait()
    spread(arrow, to_target)
    near = [None] * 3
    for at in order:
        parts = PARTS[at][1]

        def put_grad(block, part, start, line):
            rows = pl.ds(pl.multiple_of(block * width + start, tall), tall)
            grads[at][rows, lanes((part * NEAR + slot) * edges, edges)] = (line * scale).astype(bf16)

        rotate(at, put_grad)
        spots = [
            grads[at].at[:, lanes((part * NEAR + slot) * edges, edges)] for part in range(parts)
        ]
        near[at] = [
            [links.start(spot, spot, flip(4)) for spot in spots],
            [links.start(spot, spot, flip(1)) for spot in spots],
        ]

    whole = own_squares
    for index, copy in enumerate(summed):
        copy.wait_recv()
        whole = whole + square_in[index, :1, :]
    inverse = lax.rsqrt(whole / (terms * channels) + EPSILON)
    for degree in range(5):

        def normal(term, unused):
            normed[term] = (values[term].astype(f32) * inverse * gains[degree]).astype(bf16)
            return unused

        lax.fori_loop(degree * degree, (degree + 1) * (degree + 1), normal, 0)

    def edge_of(term, unused):
        value = turned(to_face, normed[term]).astype(bf16)
        face_out[:, :, lanes(term * width, width)] = value.reshape(2, halo, width)
        return unused

    lax.fori_loop(0, terms, edge_of, 0)
    halos = [
        links.start(face_out.at[1], face_in.at[0], after),
        links.start(face_out.at[0], face_in.at[1], before),
    ]
    spread(normed, to_source)

    for at in (1, 2):
        blocks = PARTS[at][0]
        height = blocks * width
        g = grads[at]
        plus = g[:, lanes(slot * edges, edges)]
        minus = g[:, lanes((NEAR + slot) * edges, edges)]
        doubled[at][:height, :edges] = plus
        doubled[at][:height, edges:] = minus
        doubled[at][height:, :edges] = minus
        doubled[at][height:, edges:] = -plus

    def backed(at, row, share_at):
        if at == 0:
            right = grads[0][:, lanes(slot * edges, edges)]
        else:
            right = doubled[at][...]
        left = weights[at][..., lanes(row * channels + share_at * width, width)]
        return across(left.reshape(-1, width), right)

    def back_leave(at):
        loads[at].wait()
        for index, peer in enumerate(peers):

            def one(row, unused):
                back_out[at][index, row] = backed(at, row, peer).astype(bf16)
                return unused

            lax.fori_loop(0, PARTS[at][0], one, 0)

    def back_send(at):
        return [
            links.start(back_out[at].at[index], back_in[at].at[index], (me, peer))
            for index, peer in enumerate(peers)
        ]

    def back_keep(at):
        first, (blocks, parts) = FIRSTS[at], PARTS[at]

        def one(row, unused):
            value = backed(at, row, share)
            for part in range(parts):
                back[first + part * blocks + row] = value[:, part * edges : (part + 1) * edges]
            return unused

        lax.fori_loop(0, blocks, one, 0)

    back_leave(1)
    for copy in halos:
        copy.wait_recv()

    def joined(term, unused):
        value = face_in[:, :, lanes(term * width, width)].reshape(2 * halo, width)
        work[term] += across(value, to_halo)
        return unused

    lax.fori_loop(0, terms, joined, 0)
    gathered = [None] * 3
    scattered = [None] * 3
    for at in order:
        blocks, parts = PARTS[at]

        def put_frame(block, part, start, line):
            rows = pl.ds(pl.multiple_of(block * channels + share * width + start, tall), tall)
            frames[at][rows, part * edges : (part + 1) * edges] = line.astype(bf16)

        rotate(at, put_frame)
        ours = frames[at].reshape(blocks, shares, width, parts * edges).at[:, share]
        gathered[at] = [links.start(ours, ours, (me, peer)) for peer in peers]

    def relay(at):
        relays = []
        for part, copy in enumerate(near[at][0]):
            copy.wait_recv()
            spot = grads[at].at[:, lanes((part * NEAR + (1 - pair) * 2 + low) * edges, edges)]
            relays.append(links.start(spot, spot, flip(1)))
        near[at].append(relays)

    scattered[1] = back_send(1)
    relay(1)
    back_leave(0)
    scattered[0] = back_send(0)
    relay(0)
    arrivals = [None] * 3

    def scatter_frames(at):
        for copy in gathered[at]:
            copy.wait_recv()
        parts = PARTS[at][1]
        short = nears[at].shape[2] // parts
        cut = frames[at].reshape(2, 2, 2, 2, short, parts * edges)
        waits = []
        for part in range(parts):
            here = nears[at].at[:, :, pl.ds(0, short), lanes((part * NEAR + slot) * edges, edges)]
            spread_lanes = pl.ds(part * edges, edges)
            for bit in (4, 5, 1):
                its_pair = 1 - pair if bit & 4 else pair
                its_low = 1 - low if bit & 1 else low
                piece = cut.at[:, its_pair, :, its_low, :, spread_lanes]
                waits.append(links.start(piece, here, flip(bit)).wait_recv)
            waits.append(bring(cut.at[:, pair, :, low, :, spread_lanes], here).wait)
        arrivals[at] = waits

    def mix(at):
        first, (blocks, parts) = FIRSTS[at], PARTS[at]

        def one(row, unused):
            if parts == 1:
                work[first + row] = product(weights[at][row], frames[at][...])
            else:
                real = product(weights[at][0, row], frames[at][...])
                imag = product(weights[at][1, row], frames[at][...])
                work[first + row] = real[:, :edges] - imag[:, edges:]
                work[first + blocks + row] = real[:, edges:] + imag[:, :edges]
            return unused

        lax.fori_loop(0, blocks, one, 0)

    def grown(at, step, one_side):
        tile = min(256, grads[at].shape[0])
        left = nears[at][:, one_side].reshape(-1, nears[at].shape[3])
        right = grads[at][pl.ds(pl.multiple_of(step * tile, tile), tile), :]
        return turned(left, right).reshape(2, -1, tile), lanes(step * tile, tile)

    aside = [None] * 3
    away = [None] * 3

    def grow_leave(at):
        for arrive in arrivals[at]:
            arrive()
        for group in near[at][1:]:
            for copy in group:
                copy.wait_recv()
        parts = PARTS[at][1]
        f, span = nears[at], NEAR * edges
        short = f.shape[2] // parts
        if parts == 2:
            for one_far in range(2):
                for one_side in range(2):
                    f[one_far, one_side, short:, :span] = -f[one_far, one_side, :short, span:]
                    f[one_far, one_side, short:, span:] = f[one_far, one_side, :short, :span]

        def leave(step, unused):
            value, columns = grown(at, step, 1 - side)
            leaving[at][:, :, columns] = value.astype(bf16)
            return unused

        lax.fori_loop(0, grads[at].shape[0] // min(256, grads[at].shape[0]), leave, 0)
        aside[at] = [
            links.start(leaving[at].at[1 - far], arriving[at].at[1 - far], flip(2))
        ]

    def grow_later(at):
        aside[at].append(links.start(leaving[at].at[far], arriving[at].at[far], flip(2)))

    def grow_keep(at):
        def stay(step, unused):
            value, columns = grown(at, step, side)
            kept[at][:, :, columns] = value
            return unused

        lax.fori_loop(0, grads[at].shape[0] // min(256, grads[at].shape[0]), stay, 0)

    def pass_on(at):
        aside[at][0].wait_recv()
        links.settle(aside[at][0])
        total = kept[at][1 - far] + arriving[at][1 - far].astype(f32)
        leaving[at][1 - far] = total.astype(bf16)
        away[at] = links.start(leaving[at].at[1 - far], final[at], flip(8))

    scatter_frames(1)
    back_leave(2)
    scattered[2] = back_send(2)
    relay(2)
    scatter_frames(0)
    grow_leave(1)
    scatter_frames(2)
    grow_keep(1)
    back_keep(1)
    mix(1)
    grow_leave(0)
    pass_on(1)
    grow_keep(0)
    mix(0)
    grow_leave(2)
    for at in order:
        grow_later(at)
    grow_keep(2)
    pass_on(0)
    mix(2)
    back_keep(0)
    back_keep(2)

    def unturn(origin, factor, put):
        def one(step, unused):
            rows = pl.ds(pl.multiple_of(step * tall, tall), tall)
            for degree in range(5):
                members = [row for row, entry in enumerate(FRAME) if entry[0] == degree]
                lines = [origin[row, rows, :] for row in members]
                if factor is not None:
                    lines = [line * factor for line in lines]
                for column in range(degree * degree, (degree + 1) * (degree + 1)):
                    value = None
                    for row, line in zip(members, lines):
                        term = rot[row, column : column + 1, :] * line
                        value = term if value is None else value + term
                    put(column, rows, value)
            return unused

        lax.fori_loop(0, width // tall, one, 0)

    def put_normed(column, rows, value):
        normed[column, rows, :] = value.astype(bf16)

    unturn(work, scale, put_normed)

    def updated(term, unused):
        arrow[term] = turned(normed[term], to_target).astype(bf16)
        return unused

    lax.fori_loop(0, terms, updated, 0)
    stored = [bring(arrow, update)]
    pass_on(2)

    for at in order:
        first, (blocks, parts) = FIRSTS[at], PARTS[at]
        for index, copy in enumerate(scattered[at]):
            copy.wait_recv()

            def add(row, unused):
                arrived = back_in[at][index, row].astype(f32)
                for part in range(parts):
                    back[first + part * blocks + row] += arrived[
                        :, part * edges : (part + 1) * edges
                    ]
                return unused

            lax.fori_loop(0, blocks, add, 0)
    unturn(back, None, put_normed)

    def end_of(term, unused):
        value = turned(to_halo, normed[term]).astype(bf16)
        ends_out[:, :, lanes(term * width, width)] = value.reshape(2, halo, width)
        return unused

    lax.fori_loop(0, terms, end_of, 0)
    ends = [
        links.start(ends_out.at[1], ends_in.at[0], after),
        links.start(ends_out.at[0], ends_in.at[1], before),
    ]

    def owned(term, unused):
        work[term] = turned(normed[term], to_source)
        return unused

    lax.fori_loop(0, terms, owned, 0)
    for copy in ends:
        copy.wait_recv()
    total = jnp.zeros((width, atoms), f32)
    for degree in range(5):

        def scaled(term, total):
            value = ends_in[:, :, lanes(term * width, width)].reshape(2 * halo, width)
            result = (work[term] + across(value, to_face)) * inverse * gains[degree]
            work[term] = result
            return total + result * values[term].astype(f32)

        total = lax.fori_loop(degree * degree, (degree + 1) * (degree + 1), scaled, total)
    whole = jnp.sum(total, axis=0, keepdims=True)
    tally_out[...] = jnp.broadcast_to(whole, tally_out.shape)
    tallies = [
        links.start(tally_out, tally_in.at[index], (me, peer))
        for index, peer in enumerate(peers)
    ]
    for index, copy in enumerate(tallies):
        copy.wait_recv()
        whole = whole + tally_in[index, :1, :]
    factor = inverse * inverse * whole / (terms * channels)

    def finished(term, unused):
        normed[term] = (work[term] - values[term].astype(f32) * factor).astype(bf16)
        return unused

    lax.fori_loop(0, terms, finished, 0)
    stored.append(bring(normed, grad_embed))
    for at in order:
        aside[at][1].wait_recv()
        total = kept[at][far] + arriving[at][far].astype(f32)
        away[at].wait_recv()
        kept[at][far] = total + final[at][...].astype(f32)
        stored.append(bring(kept[at].at[far], outs[at]))
    links.finish()
    for copy in stored:
        copy.wait()


def run_layer(arrays, sizes):
    embed, w_zero, w_one, w_two = arrays[0], arrays[3], arrays[4], arrays[5]
    shares, count = sizes
    terms, width, atoms = embed.shape
    edges, halo = arrays[8].shape[1], arrays[7].shape[1] // 2
    channels = width * shares
    cuts = (w_zero.shape[2] // count, w_one.shape[3] // count, w_two.shape[3] // count)
    bf16, f32 = jnp.bfloat16, jnp.float32
    three = range(3)
    tall = [blocks * width for blocks, parts in PARTS]
    wide = [parts * cut for (blocks, parts), cut in zip(PARTS, cuts)]
    near = [NEAR * parts * edges for blocks, parts in PARTS]
    scratch = [(w.shape, bf16) for w in (w_zero, w_one, w_two)]
    scratch += [((blocks * channels, parts * edges), bf16) for blocks, parts in PARTS]
    scratch += [((tall[i], near[i]), bf16) for i in three]
    scratch += [((2 * tall[i], 2 * edges), bf16) for i in (1, 2)]
    scratch += [((2, 2, wide[i], near[i]), bf16) for i in three]
    scratch += 2 * [
        ((shares - 1, blocks, width, parts * edges), bf16) for blocks, parts in PARTS
    ]
    scratch += [((2, wide[i], tall[i]), f32) for i in three]
    scratch += 2 * [((2, wide[i], tall[i]), bf16) for i in three]
    scratch += [((wide[i], tall[i]), bf16) for i in three]
    scratch += [
        ((terms, width, edges), f32),
        ((len(FRAME), width, edges), f32),
        ((terms, width, atoms), bf16),
        ((terms, width, atoms), bf16),
        ((terms, width, atoms), bf16),
        ((len(FRAME), terms, edges), f32),
        ((5, width, atoms), f32),
    ]
    scratch += 4 * [((2, halo, terms * width), bf16)]
    scratch += 2 * [((8, atoms), f32), ((shares - 1, 8, atoms), f32)]
    number = 8 * (shares - 1) + 15 + 15 + 9 + 4
    anywhere = pl.BlockSpec(memory_space=pl.ANY)
    inside = pl.BlockSpec(memory_space=pltpu.VMEM)
    return pl.pallas_call(
        functools.partial(layer_kernel, shares, count),
        in_specs=[anywhere] * 2 + [inside] + [anywhere] * 3 + [inside] * 6,
        out_specs=[anywhere] * 5,
        out_shape=[jax.ShapeDtypeStruct(embed.shape, bf16)] * 2
        + [jax.ShapeDtypeStruct((wide[i], tall[i]), f32) for i in three],
        scratch_shapes=[pltpu.VMEM(shape, kind) for shape, kind in scratch]
        + [
            pltpu.SemaphoreType.DMA((number,)),
            pltpu.SemaphoreType.DMA((number,)),
            pltpu.SemaphoreType.DMA((24,)),
        ],
        compiler_params=pltpu.CompilerParams(
            collective_id=0, has_side_effects=True, vmem_limit_bytes=67043328
        ),
    )(*arrays)


def shards(
    embed,
    gain,
    w_zero,
    w_one,
    w_two,
    rot_table,
    face_atoms,
    edge_source,
    edge_target,
    rot_index,
    edge_weight,
    cotangent,
):
    atoms = embed.shape[2]
    local = embed.shape[1]
    halo = face_atoms.shape[0] // 2
    shares = lax.axis_size("chan")
    channels = local * shares
    weights = (w_zero, w_one, w_two)
    values = embed.astype(jnp.float32)
    gains = gain_rows(gain)
    rows, coefficients, rots = rot_table.shape
    which = (jnp.arange(rots, dtype=jnp.int32)[:, None] == rot_index[None, :]).astype(jnp.float32)
    rotations = jnp.dot(
        rot_table.reshape(rows * coefficients, rots),
        which,
        precision=HIGHEST,
        preferred_element_type=jnp.float32,
    )
    weight_row = edge_weight[None, :]
    ones = jnp.ones_like(weight_row)

    squares = lax.psum(jnp.sum(values * values, axis=(0, 1)), "chan")
    inverse = lax.rsqrt(squares / (25 * channels) + EPSILON)
    normed = (values * inverse[None, None, :] * gains[:, :, None]).astype(jnp.bfloat16)
    flat = normed.reshape(25 * local, atoms)
    faces = product(flat, hot_rows(atoms, face_atoms)).astype(jnp.bfloat16)
    table_end = from_beside(faces.reshape(25, local, 2 * halo), halo)

    grads = to_frames([(cotangent, hot_rows(atoms, edge_target))], rotations, weight_row)
    picks = hot_rows(atoms + 2 * halo, edge_source)
    own = to_frames([(normed, picks[:atoms]), (table_end, picks[atoms:])], rotations, ones)
    own, grads = lax.optimization_barrier((own, grads))
    piece = lax.all_gather(own, "chan", axis=1, tiled=True)

    grads_side = swap(grads, 2)
    pair = swap(jnp.stack([grads, grads_side]), 1)
    grads_all = [grads, grads_side, pair[0], pair[1]]

    back = lax.psum_scatter(
        mix_back(weights, grads, shares), "chan", scatter_dimension=0, tiled=False
    )
    frames, widths = column_frames(piece)
    mixed = mix_forward(weights, piece)
    mixed, frames = lax.optimization_barrier((mixed, frames))
    (update,) = to_atoms(
        mixed, rotations, weight_row, [hot_columns(edge_target, atoms)], [jnp.bfloat16]
    )
    leaving = hot_columns(edge_source, atoms + 2 * halo)
    mine, outward = to_atoms(
        back,
        rotations,
        ones,
        [leaving[:, :atoms], leaving[:, atoms:]],
        [jnp.float32, jnp.bfloat16],
    )
    incoming = from_beside(outward, halo)
    settled = product(incoming.reshape(25 * local, 2 * halo), hot_columns(face_atoms, atoms))
    grad_normed = mine + settled.reshape(25, local, atoms)
    scaled = inverse[None, None, :] * gains[:, :, None] * grad_normed
    tally = lax.psum(jnp.sum(values * scaled, axis=(0, 1)), "chan")
    grad_embed = (
        scaled
        - values * (inverse**2 * tally / (25 * channels))[None, None, :]
    ).astype(jnp.bfloat16)
    grad_zero, grad_one, grad_two = weight_grads(frames, widths, grads_all, local)
    return (update, grad_embed, grad_zero, grad_one, grad_two)


def shards_linked(
    embed,
    gain,
    w_zero,
    w_one,
    w_two,
    rot_table,
    face_atoms,
    edge_source,
    edge_target,
    rot_index,
    edge_weight,
    cotangent,
):
    local = embed.shape[1]
    arrays = (
        embed,
        cotangent,
        gain,
        w_zero,
        w_one,
        w_two,
        rot_table,
        face_atoms[None, :],
        edge_source[None, :],
        edge_target[None, :],
        rot_index[None, :],
        edge_weight[None, :],
    )
    sizes = (lax.axis_size("chan"), lax.axis_size("graph"))
    update, grad_embed, done_zero, done_one, done_two = run_layer(arrays, sizes)
    grad_zero = jnp.transpose(done_zero).reshape(5, local, -1)
    grad_one, grad_two = [
        jnp.transpose(done.reshape(2, -1, done.shape[1]), (0, 2, 1)).reshape(2, blocks, local, -1)
        for done, blocks in ((done_one, 4), (done_two, 3))
    ]
    return (update, grad_embed, grad_zero, grad_one, grad_two)


def solution(mesh):
    placed = (
        P(None, "chan", "graph"),
        P(None, "chan"),
        P(None, "chan", None),
        P(None, None, "chan", None),
        P(None, None, "chan", None),
        P(),
        P("graph"),
        P("graph"),
        P("graph"),
        P("graph"),
        P("graph"),
        P(None, "chan", "graph"),
    )
    linked = mesh.shape["graph"] == 16 and mesh.shape["chan"] == 2
    return jax.shard_map(
        shards_linked if linked else shards,
        mesh=mesh,
        in_specs=placed,
        out_specs=(
            P(None, "chan", "graph"),
            P(None, "chan", "graph"),
            P(None, "chan", "graph"),
            P(None, None, "chan", "graph"),
            P(None, None, "chan", "graph"),
        ),
        check_vma=False,
    )
```

profile of v0, /device:TPU:18, one launch (start us, length us, event | category | flops | bytes accessed | tf_op | source)
XLA Modules:
  0.0 163.8 jit_solution(10844940788376058292)
XLA Ops:
  0.6 2.1 %copy.20.refs_6_ = f32[19,25,256]{2,1,0:T(8,128)} copy(f32[19,25,256]{2,0,1:T(8,128)} %param.17) | data formatting | bytes 972800 | tf_op args[5]
  2.7 152.3 %shard_map.155 = (bf16[25,256,128]{2,1,0:T(8,128)(2,1)}, bf16[25,256,128]{2,1,0:T(8,128)(2,1)}, f32[160,1280]{1,0:T(8,128)}, f32[256,1024]{1,0:T(8,128)}, f32[192,768]{1,0:T(8,128)}) custom-call(bf16[25,256,128]{2,1,0:T(8,128)(2,1)} %refs_0_.1, bf16[25,256,128]{2,1,0:T(8,128)(2,1)} %refs_1_.1, f32[5,256]{1,0:T(8,128)} %refs_2_.1, ...), custom_call_target="tpu_custom_call" | custom-call | tf_op jit(solution)/shard_map/pallas_call | solution.py:841
  155.0 0.0 copy-start.2
  155.0 2.0 %copy.29 = f32[2,12,3,8,256]{4,3,1,2,0:T(8,128)} copy(f32[2,12,3,8,256]{4,3,2,1,0:T(8,128)} %bitcast.26) | data formatting | bytes 1179648 | tf_op jit(solution)/shard_map/reshape | solution.py:972
  157.0 0.0 copy-start.1
  157.0 2.2 %copy.28 = f32[20,5,8,256]{3,2,0,1:T(8,128)} copy(f32[20,5,8,256]{3,2,1,0:T(8,128)} %bitcast.24) | data formatting | bytes 1638400 | tf_op jit(solution)/shard_map/reshape | solution.py:970
  159.3 0.0 copy-done.2
  159.3 1.3 copy.21
  160.6 0.0 copy-done.1
  160.6 0.0 copy-start
  160.6 1.2 copy.32
  161.7 0.9 copy-done
  162.6 1.2 copy.33
Async XLA Ops:
  155.0 4.3 %copy-start.2 = (f32[256,1024]{1,0:T(8,128)S(1)}, f32[256,1024]{1,0:T(8,128)}, u32[]{:S(2)}) copy-start(f32[256,1024]{1,0:T(8,128)} %get-tuple-element.13) | copy-start | bytes 3145732
  157.0 3.5 %copy-start.1 = (bf16[25,256,128]{2,1,0:T(8,128)(2,1)S(1)}, bf16[25,256,128]{2,1,0:T(8,128)(2,1)}, u32[]{:S(2)}) copy-start(bf16[25,256,128]{2,1,0:T(8,128)(2,1)} %get-tuple-element.30) | copy-start | bytes 4915204
  160.6 2.0 %copy-start = (bf16[25,256,128]{2,1,0:T(8,128)(2,1)S(1)}, bf16[25,256,128]{2,1,0:T(8,128)(2,1)}, u32[]{:S(2)}) copy-start(bf16[25,256,128]{2,1,0:T(8,128)(2,1)} %get-tuple-element.31) | copy-start | bytes 4915204
where the time goes:
time: 164 us
  Pallas kernels  152 us (93%)
  local copies, waits for them, and re-layouts  10.8 us (7%)
    pallas_call x1, Pallas kernels, run_layer(): pl.pallas_call(functools.partial(layer_kernel, shares, count), in_specs=[...  152 us
    unnamed x9, local copies, waits for them, and re-layouts  5.26 us

commit v1 on v0

--- a/solution.py
+++ b/solution.py
@@ -352,6 +352,7 @@
     share = lax.axis_index("chan")
     low, side, pair, far = me % 2, (me // 2) % 2, (me // 4) % 2, (me // 8) % 2
     slot = pair * 2 + low
+    batch = 5
 
     def flip(bit):
         digits = {1: low, 2: side, 4: pair, 8: far}
@@ -384,16 +385,34 @@
             barrier, inc=1, device_id=other, device_id_type=pl.DeviceIdType.MESH
         )
     links = Links(sends, recvs)
-
-    which = hot(table.shape[2], which_row[...]).astype(f32)
-
-    def turn(row, unused):
-        rot[row] = jnp.dot(
-            table[row], which, precision=HIGHEST, preferred_element_type=f32
-        )
+    load_embed.wait()
+
+    def squared(term, total):
+        value = values[term].astype(f32)
+        return total + value * value
+
+    total = lax.fori_loop(0, terms, squared, jnp.zeros((width, atoms), f32))
+    own_squares = jnp.sum(total, axis=0, keepdims=True)
+    square_out[...] = jnp.broadcast_to(own_squares, square_out.shape)
+    pl.semaphore_wait(barrier, len(others))
+    summed = [
+        links.start(square_out, square_in.at[index], (me, peer))
+        for index, peer in enumerate(peers)
+    ]
+
+    which = hot(table.shape[2], which_row[...])
+
+    def turn(term, unused):
+        rest, total = table[term], None
+        for _ in range(3):
+            part = rest.astype(bf16)
+            rest = rest - part.astype(f32)
+            value = product(part, which)
+            total = value if total is None else total + value
+        rot[term] = total
         return unused
 
-    lax.fori_loop(0, len(FRAME), turn, 0)
+    lax.fori_loop(0, terms, turn, 0, unroll=5)
     degrees = lax.broadcasted_iota(jnp.int32, (5, atoms), 0)
     for degree in range(5):
         gains[degree] = lax.dot_general(
@@ -412,27 +431,52 @@
     to_face = turned(unit, faces).astype(bf16)
     scale = weight_row[...]
 
-    load_embed.wait()
-
-    def squared(term, total):
-        value = values[term].astype(f32)
-        return total + value * value
-
-    total = lax.fori_loop(0, terms, squared, jnp.zeros((width, atoms), f32))
-    own_squares = jnp.sum(total, axis=0, keepdims=True)
-    square_out[...] = jnp.broadcast_to(own_squares, square_out.shape)
-    pl.semaphore_wait(barrier, len(others))
-    summed = [
-        links.start(square_out, square_in.at[index], (me, peer))
-        for index, peer in enumerate(peers)
+    whole = own_squares
+    for index, copy in enumerate(summed):
+        copy.wait_recv()
+        whole = whole + square_in[index, :1, :]
+    inverse = lax.rsqrt(whole / (terms * channels) + EPSILON)
+    for degree in range(5):
+
+        def normal(term, unused):
+            normed[term] = (values[term].astype(f32) * inverse * gains[degree]).astype(bf16)
+            return unused
+
+        lax.fori_loop(degree * degree, (degree + 1) * (degree + 1), normal, 0)
+
+    def fold(picks, target):
+        def one(step, unused):
+            value = normed[pl.ds(step * batch, batch)].reshape(batch * width, atoms)
+            value = turned(picks, value).astype(bf16).reshape(2, halo, batch * width)
+            target[:, :, lanes(step * batch * width, batch * width)] = value
+            return unused
+
+        lax.fori_loop(0, terms // batch, one, 0)
+
+    def unfold(origin, picks):
+        def one(step, unused):
+            some = pl.ds(step * batch, batch)
+            value = origin[:, :, lanes(step * batch * width, batch * width)]
+            value = across(value.reshape(2 * halo, batch * width), picks)
+            work[some] += value.reshape(batch, width, atoms)
+            return unused
+
+        lax.fori_loop(0, terms // batch, one, 0)
+
+    fold(to_face, face_out)
+    halos = [
+        links.start(face_out.at[1], face_in.at[0], after),
+        links.start(face_out.at[0], face_in.at[1], before),
     ]
 
     def spread(values_ref, picks):
-        def one(term, unused):
-            work[term] = product(values_ref[term], picks)
-            return unused
-
-        lax.fori_loop(0, terms, one, 0)
+        def one(step, unused):
+            some = pl.ds(step * batch, batch)
+            value = values_ref[some].reshape(batch * width, atoms)
+            work[some] = product(value, picks).reshape(batch, width, edges)
+            return unused
+
+        lax.fori_loop(0, terms // batch, one, 0)
 
     tall = min(32, width)
 
@@ -454,7 +498,7 @@
                 for row in members:
                     line = None
                     for index, entry in enumerate(lines):
-                        term = rot[row, base + index : base + index + 1, :] * entry
+                        term = rot[base + index, row : row + 1, :] * entry
                         line = term if line is None else line + term
                     part, block = divmod(row - first, blocks)
                     put(block, part, step * tall, line)
@@ -465,47 +509,27 @@
     load_cotangent.wait()
     spread(arrow, to_target)
     near = [None] * 3
-    for at in order:
-        parts = PARTS[at][1]
-
-        def put_grad(block, part, start, line):
-            rows = pl.ds(pl.multiple_of(block * width + start, tall), tall)
-            grads[at][rows, lanes((part * NEAR + slot) * edges, edges)] = (line * scale).astype(bf16)
-
-        rotate(at, put_grad)
+
+    def near_send(at):
         spots = [
-            grads[at].at[:, lanes((part * NEAR + slot) * edges, edges)] for part in range(parts)
+            grads[at].at[:, lanes((part * NEAR + slot) * edges, edges)]
+            for part in range(PARTS[at][1])
         ]
         near[at] = [
             [links.start(spot, spot, flip(4)) for spot in spots],
             [links.start(spot, spot, flip(1)) for spot in spots],
         ]
 
-    whole = own_squares
-    for index, copy in enumerate(summed):
-        copy.wait_recv()
-        whole = whole + square_in[index, :1, :]
-    inverse = lax.rsqrt(whole / (terms * channels) + EPSILON)
-    for degree in range(5):
-
-        def normal(term, unused):
-            normed[term] = (values[term].astype(f32) * inverse * gains[degree]).astype(bf16)
-            return unused
-
-        lax.fori_loop(degree * degree, (degree + 1) * (degree + 1), normal, 0)
-
-    def edge_of(term, unused):
-        value = turned(to_face, normed[term]).astype(bf16)
-        face_out[:, :, lanes(term * width, width)] = value.reshape(2, halo, width)
-        return unused
-
-    lax.fori_loop(0, terms, edge_of, 0)
-    halos = [
-        links.start(face_out.at[1], face_in.at[0], after),
-        links.start(face_out.at[0], face_in.at[1], before),
-    ]
+    for at in order:
+
+        def put_grad(block, part, start, line):
+            rows = pl.ds(pl.multiple_of(block * width + start, tall), tall)
+            grads[at][rows, lanes((part * NEAR + slot) * edges, edges)] = (line * scale).astype(bf16)
+
+        rotate(at, put_grad)
+        if at == 1:
+            near_send(1)
     spread(normed, to_source)
-
     for at in (1, 2):
         blocks = PARTS[at][0]
         height = blocks * width
@@ -535,8 +559,10 @@
 
             lax.fori_loop(0, PARTS[at][0], one, 0)
 
+    scattered = [None] * 3
+
     def back_send(at):
-        return [
+        scattered[at] = [
             links.start(back_out[at].at[index], back_in[at].at[index], (me, peer))
             for index, peer in enumerate(peers)
         ]
@@ -551,29 +577,6 @@
             return unused
 
         lax.fori_loop(0, blocks, one, 0)
-
-    back_leave(1)
-    for copy in halos:
-        copy.wait_recv()
-
-    def joined(term, unused):
-        value = face_in[:, :, lanes(term * width, width)].reshape(2 * halo, width)
-        work[term] += across(value, to_halo)
-        return unused
-
-    lax.fori_loop(0, terms, joined, 0)
-    gathered = [None] * 3
-    scattered = [None] * 3
-    for at in order:
-        blocks, parts = PARTS[at]
-
-        def put_frame(block, part, start, line):
-            rows = pl.ds(pl.multiple_of(block * channels + share * width + start, tall), tall)
-            frames[at][rows, part * edges : (part + 1) * edges] = line.astype(bf16)
-
-        rotate(at, put_frame)
-        ours = frames[at].reshape(blocks, shares, width, parts * edges).at[:, share]
-        gathered[at] = [links.start(ours, ours, (me, peer)) for peer in peers]
 
     def relay(at):
         relays = []
@@ -583,30 +586,42 @@
             relays.append(links.start(spot, spot, flip(1)))
         near[at].append(relays)
 
-    scattered[1] = back_send(1)
-    relay(1)
-    back_leave(0)
-    scattered[0] = back_send(0)
-    relay(0)
-    arrivals = [None] * 3
-
-    def scatter_frames(at):
-        for copy in gathered[at]:
+    gathered = {}
+
+    def share_frames(at, turn_at):
+        blocks, parts = PARTS[at]
+        size = (blocks + 1) // 2
+        if turn_at == 0:
+            start = (1 - far) * (blocks - size)
+        else:
+            start, size = far * size, blocks - size
+        ours = frames[at].reshape(blocks, shares, width, parts * edges)
+        ours = ours.at[pl.ds(start, size), share]
+        gathered[at, turn_at] = [links.start(ours, ours, (me, peer)) for peer in peers]
+
+    arrivals = {}
+    places = (1 - far, far)
+
+    def scatter(at, turn_at):
+        for copy in gathered[at, turn_at]:
             copy.wait_recv()
         parts = PARTS[at][1]
+        place = places[turn_at]
         short = nears[at].shape[2] // parts
         cut = frames[at].reshape(2, 2, 2, 2, short, parts * edges)
         waits = []
         for part in range(parts):
-            here = nears[at].at[:, :, pl.ds(0, short), lanes((part * NEAR + slot) * edges, edges)]
+            here = nears[at].at[
+                place, :, pl.ds(0, short), lanes((part * NEAR + slot) * edges, edges)
+            ]
             spread_lanes = pl.ds(part * edges, edges)
             for bit in (4, 5, 1):
                 its_pair = 1 - pair if bit & 4 else pair
                 its_low = 1 - low if bit & 1 else low
-                piece = cut.at[:, its_pair, :, its_low, :, spread_lanes]
+                piece = cut.at[place, its_pair, :, its_low, :, spread_lanes]
                 waits.append(links.start(piece, here, flip(bit)).wait_recv)
-            waits.append(bring(cut.at[:, pair, :, low, :, spread_lanes], here).wait)
-        arrivals[at] = waits
+            waits.append(bring(cut.at[place, pair, :, low, :, spread_lanes], here).wait)
+        arrivals[at, turn_at] = waits
 
     def mix(at):
         first, (blocks, parts) = FIRSTS[at], PARTS[at]
@@ -623,80 +638,118 @@
 
         lax.fori_loop(0, blocks, one, 0)
 
-    def grown(at, step, one_side):
-        tile = min(256, grads[at].shape[0])
-        left = nears[at][:, one_side].reshape(-1, nears[at].shape[3])
-        right = grads[at][pl.ds(pl.multiple_of(step * tile, tile), tile), :]
-        return turned(left, right).reshape(2, -1, tile), lanes(step * tile, tile)
-
-    aside = [None] * 3
-    away = [None] * 3
-
-    def grow_leave(at):
-        for arrive in arrivals[at]:
+    def grown(at, place, step, one_side):
+        columns = nears[at][place, one_side]
+        rows = grads[at][pl.ds(pl.multiple_of(step * width, width), width), :]
+        return turned(rows, columns) if at == 1 else turned(columns, rows)
+
+    aside = {}
+    away = {}
+    pieces = {1: ((0, 2), (2, 4)), 0: ((0, 5),), 2: ((0, 3),)}
+
+    def grow_leave(at, turn_at):
+        for arrive in arrivals[at, turn_at]:
             arrive()
-        for group in near[at][1:]:
-            for copy in group:
-                copy.wait_recv()
+        if turn_at == 0:
+            for group in near[at][1:]:
+                for copy in group:
+                    copy.wait_recv()
         parts = PARTS[at][1]
+        place = places[turn_at]
         f, span = nears[at], NEAR * edges
         short = f.shape[2] // parts
         if parts == 2:
-            for one_far in range(2):
-                for one_side in range(2):
-                    f[one_far, one_side, short:, :span] = -f[one_far, one_side, :short, span:]
-                    f[one_far, one_side, short:, span:] = f[one_far, one_side, :short, :span]
+            for one_side in range(2):
+                f[place, one_side, short:, :span] = -f[place, one_side, :short, span:]
+                f[place, one_side, short:, span:] = f[place, one_side, :short, :span]
 
         def leave(step, unused):
-            value, columns = grown(at, step, 1 - side)
-            leaving[at][:, :, columns] = value.astype(bf16)
-            return unused
-
-        lax.fori_loop(0, grads[at].shape[0] // min(256, grads[at].shape[0]), leave, 0)
-        aside[at] = [
-            links.start(leaving[at].at[1 - far], arriving[at].at[1 - far], flip(2))
-        ]
-
-    def grow_later(at):
-        aside[at].append(links.start(leaving[at].at[far], arriving[at].at[far], flip(2)))
-
-    def grow_keep(at):
+            leaving[at][place, step] = grown(at, place, step, 1 - side).astype(bf16)
+            return unused
+
+        for index, (start, stop) in enumerate(pieces[at]):
+            lax.fori_loop(start, stop, leave, 0)
+            steps = pl.ds(start, stop - start)
+            aside[at, turn_at, index] = links.start(
+                leaving[at].at[place, steps], arriving[at].at[place, steps], flip(2)
+            )
+
+    def grow_keep(at, turn_at):
+        place = places[turn_at]
+
         def stay(step, unused):
-            value, columns = grown(at, step, side)
-            kept[at][:, :, columns] = value
-            return unused
-
-        lax.fori_loop(0, grads[at].shape[0] // min(256, grads[at].shape[0]), stay, 0)
-
-    def pass_on(at):
-        aside[at][0].wait_recv()
-        links.settle(aside[at][0])
-        total = kept[at][1 - far] + arriving[at][1 - far].astype(f32)
-        leaving[at][1 - far] = total.astype(bf16)
-        away[at] = links.start(leaving[at].at[1 - far], final[at], flip(8))
-
-    scatter_frames(1)
+            kept[at][place, step] = grown(at, place, step, side)
+            return unused
+
+        lax.fori_loop(0, PARTS[at][0], stay, 0)
+
+    def pass_on(at, index):
+        start, stop = pieces[at][index]
+        aside[at, 0, index].wait_recv()
+        links.settle(aside[at, 0, index])
+        place = places[0]
+
+        def one(step, unused):
+            total = kept[at][place, step] + arriving[at][place, step].astype(f32)
+            leaving[at][place, step] = total.astype(bf16)
+            return unused
+
+        lax.fori_loop(start, stop, one, 0)
+        steps = pl.ds(start, stop - start)
+        away[at, index] = links.start(
+            leaving[at].at[place, steps], final[at].at[steps], flip(8)
+        )
+
+    back_leave(1)
+    for copy in halos:
+        copy.wait_recv()
+    unfold(face_in, to_halo)
+    for at in order:
+        blocks, parts = PARTS[at]
+
+        def put_frame(block, part, start, line):
+            rows = pl.ds(pl.multiple_of(block * channels + share * width + start, tall), tall)
+            frames[at][rows, part * edges : (part + 1) * edges] = line.astype(bf16)
+
+        rotate(at, put_frame)
+        share_frames(at, 0)
+    for at in order:
+        share_frames(at, 1)
+    back_send(1)
+    back_leave(0)
+    back_send(0)
+    relay(1)
+    scatter(1, 0)
+    near_send(0)
     back_leave(2)
-    scattered[2] = back_send(2)
-    relay(2)
-    scatter_frames(0)
-    grow_leave(1)
-    scatter_frames(2)
-    grow_keep(1)
+    back_send(2)
     back_keep(1)
-    mix(1)
-    grow_leave(0)
-    pass_on(1)
-    grow_keep(0)
-    mix(0)
-    grow_leave(2)
-    for at in order:
-        grow_later(at)
-    grow_keep(2)
-    pass_on(0)
-    mix(2)
+    scatter(0, 0)
+    near_send(2)
+    grow_leave(1, 0)
+    grow_keep(1, 0)
+    scatter(2, 0)
+    relay(0)
     back_keep(0)
     back_keep(2)
+    scatter(1, 1)
+    pass_on(1, 0)
+    pass_on(1, 1)
+    relay(2)
+    scatter(0, 1)
+    grow_leave(0, 0)
+    grow_keep(0, 0)
+    scatter(2, 1)
+    mix(1)
+    grow_leave(2, 0)
+    grow_keep(2, 0)
+    pass_on(0, 0)
+    mix(0)
+    grow_leave(1, 1)
+    mix(2)
+    pass_on(2, 0)
+    grow_leave(0, 1)
+    grow_leave(2, 1)
 
     def unturn(origin, factor, put):
         def one(step, unused):
@@ -709,7 +762,7 @@
                 for column in range(degree * degree, (degree + 1) * (degree + 1)):
                     value = None
                     for row, line in zip(members, lines):
-                        term = rot[row, column : column + 1, :] * line
+                        term = rot[column, row : row + 1, :] * line
                         value = term if value is None else value + term
                     put(column, rows, value)
             return unused
@@ -721,14 +774,19 @@
 
     unturn(work, scale, put_normed)
 
-    def updated(term, unused):
-        arrow[term] = turned(normed[term], to_target).astype(bf16)
-        return unused
-
-    lax.fori_loop(0, terms, updated, 0)
+    def gather(picks, target):
+        def one(step, unused):
+            some = pl.ds(step * batch, batch)
+            value = turned(normed[some].reshape(batch * width, edges), picks)
+            target[some] = value.reshape(batch, width, atoms).astype(target.dtype)
+            return unused
+
+        lax.fori_loop(0, terms // batch, one, 0)
+
+    gather(to_target, arrow)
     stored = [bring(arrow, update)]
-    pass_on(2)
-
+    for at in order:
+        grow_keep(at, 1)
     for at in order:
         first, (blocks, parts) = FIRSTS[at], PARTS[at]
         for index, copy in enumerate(scattered[at]):
@@ -745,30 +803,21 @@
             lax.fori_loop(0, blocks, add, 0)
     unturn(back, None, put_normed)
 
-    def end_of(term, unused):
-        value = turned(to_halo, normed[term]).astype(bf16)
-        ends_out[:, :, lanes(term * width, width)] = value.reshape(2, halo, width)
-        return unused
-
-    lax.fori_loop(0, terms, end_of, 0)
+    fold(to_halo, ends_out)
     ends = [
         links.start(ends_out.at[1], ends_in.at[0], after),
         links.start(ends_out.at[0], ends_in.at[1], before),
     ]
 
-    def owned(term, unused):
-        work[term] = turned(normed[term], to_source)
-        return unused
-
-    lax.fori_loop(0, terms, owned, 0)
+    gather(to_source, work)
     for copy in ends:
         copy.wait_recv()
+    unfold(ends_in, to_face)
     total = jnp.zeros((width, atoms), f32)
     for degree in range(5):
 
         def scaled(term, total):
-            value = ends_in[:, :, lanes(term * width, width)].reshape(2 * halo, width)
-            result = (work[term] + across(value, to_face)) * inverse * gains[degree]
+            result = work[term] * inverse * gains[degree]
             work[term] = result
             return total + result * values[term].astype(f32)
 
@@ -791,11 +840,25 @@
     lax.fori_loop(0, terms, finished, 0)
     stored.append(bring(normed, grad_embed))
     for at in order:
-        aside[at][1].wait_recv()
-        total = kept[at][far] + arriving[at][far].astype(f32)
-        away[at].wait_recv()
-        kept[at][far] = total + final[at][...].astype(f32)
-        stored.append(bring(kept[at].at[far], outs[at]))
+        for index in range(len(pieces[at])):
+            aside[at, 1, index].wait_recv()
+            away[at, index].wait_recv()
+
+        def settled(step, unused):
+            total = kept[at][far, step] + arriving[at][far, step].astype(f32)
+            kept[at][far, step] = total + final[at][step].astype(f32)
+            return unused
+
+        lax.fori_loop(0, PARTS[at][0], settled, 0)
+        ready = kept[at].at[far]
+        if at == 0:
+            stored.append(bring(ready, outs[at]))
+        else:
+            for part in range(2):
+                short = outs[at].shape[-1 if at == 1 else -2]
+                some = pl.ds(part * short, short)
+                piece = ready.at[:, :, some] if at == 1 else ready.at[:, some]
+                stored.append(bring(piece, outs[at].at[part]))
     links.finish()
     for copy in stored:
         copy.wait()
@@ -821,21 +884,26 @@
     scratch += 2 * [
         ((shares - 1, blocks, width, parts * edges), bf16) for blocks, parts in PARTS
     ]
-    scratch += [((2, wide[i], tall[i]), f32) for i in three]
-    scratch += 2 * [((2, wide[i], tall[i]), bf16) for i in three]
-    scratch += [((wide[i], tall[i]), bf16) for i in three]
+    slabs = [
+        (5, wide[0], width),
+        (4, width, wide[1]),
+        (3, wide[2], width),
+    ]
+    scratch += [((2,) + slab, f32) for slab in slabs]
+    scratch += 2 * [((2,) + slab, bf16) for slab in slabs]
+    scratch += [(slab, bf16) for slab in slabs]
     scratch += [
         ((terms, width, edges), f32),
         ((len(FRAME), width, edges), f32),
         ((terms, width, atoms), bf16),
         ((terms, width, atoms), bf16),
         ((terms, width, atoms), bf16),
-        ((len(FRAME), terms, edges), f32),
+        ((terms, len(FRAME), edges), f32),
         ((5, width, atoms), f32),
     ]
     scratch += 4 * [((2, halo, terms * width), bf16)]
     scratch += 2 * [((8, atoms), f32), ((shares - 1, 8, atoms), f32)]
-    number = 8 * (shares - 1) + 15 + 15 + 9 + 4
+    number = 11 * (shares - 1) + 15 + 30 + 12 + 4
     anywhere = pl.BlockSpec(memory_space=pl.ANY)
     inside = pl.BlockSpec(memory_space=pltpu.VMEM)
     return pl.pallas_call(
@@ -843,12 +911,16 @@
         in_specs=[anywhere] * 2 + [inside] + [anywhere] * 3 + [inside] * 6,
         out_specs=[anywhere] * 5,
         out_shape=[jax.ShapeDtypeStruct(embed.shape, bf16)] * 2
-        + [jax.ShapeDtypeStruct((wide[i], tall[i]), f32) for i in three],
+        + [
+            jax.ShapeDtypeStruct((5, cuts[0], width), f32),
+            jax.ShapeDtypeStruct((2, 4, width, cuts[1]), f32),
+            jax.ShapeDtypeStruct((2, 3, cuts[2], width), f32),
+        ],
         scratch_shapes=[pltpu.VMEM(shape, kind) for shape, kind in scratch]
         + [
             pltpu.SemaphoreType.DMA((number,)),
             pltpu.SemaphoreType.DMA((number,)),
-            pltpu.SemaphoreType.DMA((24,)),
+            pltpu.SemaphoreType.DMA((32,)),
         ],
         compiler_params=pltpu.CompilerParams(
             collective_id=0, has_side_effects=True, vmem_limit_bytes=67043328
@@ -950,7 +1022,6 @@
     edge_weight,
     cotangent,
 ):
-    local = embed.shape[1]
     arrays = (
         embed,
         cotangent,
@@ -958,7 +1029,7 @@
         w_zero,
         w_one,
         w_two,
-        rot_table,
+        jnp.transpose(rot_table, (1, 0, 2)),
         face_atoms[None, :],
         edge_source[None, :],
         edge_target[None, :],
@@ -967,12 +1038,9 @@
     )
     sizes = (lax.axis_size("chan"), lax.axis_size("graph"))
     update, grad_embed, done_zero, done_one, done_two = run_layer(arrays, sizes)
-    grad_zero = jnp.transpose(done_zero).reshape(5, local, -1)
-    grad_one, grad_two = [
-        jnp.transpose(done.reshape(2, -1, done.shape[1]), (0, 2, 1)).reshape(2, blocks, local, -1)
-        for done, blocks in ((done_one, 4), (done_two, 3))
-    ]
-    return (update, grad_embed, grad_zero, grad_one, grad_two)
+    grad_zero = jnp.transpose(done_zero, (0, 2, 1))
+    grad_two = jnp.transpose(done_two, (0, 1, 3, 2))
+    return (update, grad_embed, grad_zero, done_one, grad_two)
 
 
 def solution(mesh):

time: 164 us -> 129 us (0.79)
  the two profiles are of different devices: /device:TPU:18 before, /device:TPU:25 now
where the time goes in v1:
time: 129 us; the launch traced here: 128 us
  Pallas kernels  120 us (93%)
  local copies, waits for them, and re-layouts  7.9 us (6%)
    pallas_call x1, Pallas kernels, run_layer(): pl.pallas_call(functools.partial(layer_kernel, shares, count), in_specs=[...  120 us
    unnamed x13, local copies, waits for them, and re-layouts  7.9 us

profile of v1, /device:TPU:25, one launch (start us, length us, event | category | flops | bytes accessed | tf_op | source)
XLA Modules:
  0.0 128.3 jit_solution(3984435200941384625)
XLA Ops:
  0.6 119.8 %shard_map.155 = (bf16[25,256,128]{2,1,0:T(8,128)(2,1)}, bf16[25,256,128]{2,1,0:T(8,128)(2,1)}, f32[5,160,256]{2,1,0:T(8,128)}, f32[2,4,256,128]{3,2,1,0:T(8,128)}, f32[2,3,96,256]{3,2,1,0:T(8,128)}) custom-call(bf16[25,256,128]{2,1,0:T(8,128)(2,1)} %refs_0_.1, bf16[25,256,128]{2,1,0:T(8,128)(2,1)} %refs_1_.1, f32[5,256]{1,0:T(8,128)} %refs_2_.1, ...), custom_call_target="tpu_custom_call" | custom-call | tf_op jit(solution)/shard_map/pallas_call | solution.py:909
  120.4 0.0 copy-start
  120.4 2.9 %copy.22 = bf16[25,256,128]{2,1,0:T(8,128)(2,1)} copy(bf16[25,256,128]{2,1,0:T(8,128)(2,1)} %get-tuple-element.20) | data formatting | bytes 3276800
  123.3 0.0 copy-done
  123.3 0.0 copy-start.2
  123.3 1.2 copy.23
  124.5 0.5 copy-done.2
  125.0 0.0 copy-start.1
  125.0 0.0 copy-start.3
  125.0 0.9 copy.24
  125.9 0.6 copy-done.1
  126.6 1.0 copy.25
  127.5 0.0 copy-done.3
  127.5 0.8 copy.26
Async XLA Ops:
  120.4 2.9 %copy-start = (bf16[25,256,128]{2,1,0:T(8,128)(2,1)S(1)}, bf16[25,256,128]{2,1,0:T(8,128)(2,1)}, u32[]{:S(2)}) copy-start(bf16[25,256,128]{2,1,0:T(8,128)(2,1)} %get-tuple-element.21) | copy-start | bytes 4915204
  123.3 1.7 %copy-start.2 = (f32[5,160,256]{2,1,0:T(8,128)S(1)}, f32[5,160,256]{2,1,0:T(8,128)}, u32[]{:S(2)}) copy-start(f32[5,160,256]{2,1,0:T(8,128)} %get-tuple-element.12) | copy-start | bytes 2457604
  125.0 1.5 %copy-start.1 = (f32[2,4,256,128]{3,2,1,0:T(8,128)S(1)}, f32[2,4,256,128]{3,2,1,0:T(8,128)}, u32[]{:S(2)}) copy-start(f32[2,4,256,128]{3,2,1,0:T(8,128)} %get-tuple-element.23) | copy-start | bytes 3145732
  125.0 2.5 %copy-start.3 = (f32[2,3,96,256]{3,2,1,0:T(8,128)S(1)}, f32[2,3,96,256]{3,2,1,0:T(8,128)}, u32[]{:S(2)}) copy-start(f32[2,3,96,256]{3,2,1,0:T(8,128)} %get-tuple-element.14) | copy-start | bytes 1769476

commit v2 on v1

--- a/solution.py
+++ b/solution.py
@@ -385,21 +385,6 @@
             barrier, inc=1, device_id=other, device_id_type=pl.DeviceIdType.MESH
         )
     links = Links(sends, recvs)
-    load_embed.wait()
-
-    def squared(term, total):
-        value = values[term].astype(f32)
-        return total + value * value
-
-    total = lax.fori_loop(0, terms, squared, jnp.zeros((width, atoms), f32))
-    own_squares = jnp.sum(total, axis=0, keepdims=True)
-    square_out[...] = jnp.broadcast_to(own_squares, square_out.shape)
-    pl.semaphore_wait(barrier, len(others))
-    summed = [
-        links.start(square_out, square_in.at[index], (me, peer))
-        for index, peer in enumerate(peers)
-    ]
-
     which = hot(table.shape[2], which_row[...])
 
     def turn(term, unused):
@@ -430,6 +415,21 @@
     unit = (square == lax.broadcasted_iota(jnp.int32, square.shape, 1)).astype(bf16)
     to_face = turned(unit, faces).astype(bf16)
     scale = weight_row[...]
+
+    load_embed.wait()
+
+    def squared(term, total):
+        value = values[term].astype(f32)
+        return total + value * value
+
+    total = lax.fori_loop(0, terms, squared, jnp.zeros((width, atoms), f32))
+    own_squares = jnp.sum(total, axis=0, keepdims=True)
+    square_out[...] = jnp.broadcast_to(own_squares, square_out.shape)
+    pl.semaphore_wait(barrier, len(others))
+    summed = [
+        links.start(square_out, square_in.at[index], (me, peer))
+        for index, peer in enumerate(peers)
+    ]
 
     whole = own_squares
     for index, copy in enumerate(summed):
@@ -529,7 +529,6 @@
         rotate(at, put_grad)
         if at == 1:
             near_send(1)
-    spread(normed, to_source)
     for at in (1, 2):
         blocks = PARTS[at][0]
         height = blocks * width
@@ -549,21 +548,23 @@
         left = weights[at][..., lanes(row * channels + share_at * width, width)]
         return across(left.reshape(-1, width), right)
 
-    def back_leave(at):
-        loads[at].wait()
+    scattered = {at: [] for at in order}
+
+    def back_leave(at, start, stop):
+        if start == 0:
+            loads[at].wait()
         for index, peer in enumerate(peers):
 
             def one(row, unused):
                 back_out[at][index, row] = backed(at, row, peer).astype(bf16)
                 return unused
 
-            lax.fori_loop(0, PARTS[at][0], one, 0)
-
-    scattered = [None] * 3
-
-    def back_send(at):
-        scattered[at] = [
-            links.start(back_out[at].at[index], back_in[at].at[index], (me, peer))
+            lax.fori_loop(start, stop, one, 0)
+
+    def back_send(at, start, stop):
+        rows = pl.ds(start, stop - start)
+        scattered[at] += [
+            links.start(back_out[at].at[index, rows], back_in[at].at[index, rows], (me, peer))
             for index, peer in enumerate(peers)
         ]
 
@@ -599,10 +600,50 @@
         ours = ours.at[pl.ds(start, size), share]
         gathered[at, turn_at] = [links.start(ours, ours, (me, peer)) for peer in peers]
 
-    arrivals = {}
+    arrivals, passing, through = {}, {}, {}
     places = (1 - far, far)
 
-    def scatter(at, turn_at):
+    def scatter(at, turn_at, own):
+        parts = PARTS[at][1]
+        place = places[turn_at]
+        short = nears[at].shape[2] // parts
+        cut = frames[at].reshape(2, 2, 2, 2, short, parts * edges)
+        one_side = share if own else 1 - share
+        if not own:
+            for copy in gathered[at, turn_at]:
+                copy.wait_recv()
+        waits = arrivals.setdefault((at, turn_at), [])
+        for part in range(parts):
+            spread_lanes = pl.ds(part * edges, edges)
+
+            def here(first_slot, slots):
+                start = (part * NEAR + first_slot) * edges
+                return nears[at].at[
+                    place, one_side, pl.ds(0, short), lanes(start, slots * edges)
+                ]
+
+            for bit in (4, 5, 1) if own else (1,):
+                its_pair = 1 - pair if bit & 4 else pair
+                its_low = 1 - low if bit & 1 else low
+                piece = cut.at[place, its_pair, one_side, its_low, :, spread_lanes]
+                copy = links.start(piece, here(slot, 1), flip(bit))
+                if bit & 4:
+                    passing.setdefault((at, turn_at, part), []).append(copy)
+                else:
+                    waits.append(copy.wait_recv)
+            piece = cut.at[place, pair, one_side, low, :, spread_lanes]
+            waits.append(bring(piece, here(slot, 1)).wait)
+            if own:
+                through[at, turn_at, part] = here((1 - pair) * 2, 2)
+
+    def forward(at, turn_at):
+        for part in range(PARTS[at][1]):
+            for copy in passing[at, turn_at, part]:
+                copy.wait_recv()
+            spot = through[at, turn_at, part]
+            arrivals[at, turn_at].append(links.start(spot, spot, (me, peers[0])).wait_recv)
+
+    def scatter_both(at, turn_at):
         for copy in gathered[at, turn_at]:
             copy.wait_recv()
         parts = PARTS[at][1]
@@ -645,7 +686,7 @@
 
     aside = {}
     away = {}
-    pieces = {1: ((0, 2), (2, 4)), 0: ((0, 5),), 2: ((0, 3),)}
+    pieces = {1: ((0, 1), (1, 2), (2, 3), (3, 4)), 0: ((0, 3), (3, 5)), 2: ((0, 3),)}
 
     def grow_leave(at, turn_at):
         for arrive in arrivals[at, turn_at]:
@@ -700,56 +741,25 @@
             leaving[at].at[place, steps], final[at].at[steps], flip(8)
         )
 
-    back_leave(1)
+    back_leave(1, 0, 2)
+    back_send(1, 0, 2)
+    spread(normed, to_source)
+    back_leave(1, 2, 4)
     for copy in halos:
         copy.wait_recv()
     unfold(face_in, to_halo)
     for at in order:
-        blocks, parts = PARTS[at]
+        blocks, _ = PARTS[at]
 
         def put_frame(block, part, start, line):
             rows = pl.ds(pl.multiple_of(block * channels + share * width + start, tall), tall)
             frames[at][rows, part * edges : (part + 1) * edges] = line.astype(bf16)
 
         rotate(at, put_frame)
-        share_frames(at, 0)
-    for at in order:
-        share_frames(at, 1)
-    back_send(1)
-    back_leave(0)
-    back_send(0)
-    relay(1)
-    scatter(1, 0)
-    near_send(0)
-    back_leave(2)
-    back_send(2)
-    back_keep(1)
-    scatter(0, 0)
-    near_send(2)
-    grow_leave(1, 0)
-    grow_keep(1, 0)
-    scatter(2, 0)
-    relay(0)
-    back_keep(0)
-    back_keep(2)
-    scatter(1, 1)
-    pass_on(1, 0)
-    pass_on(1, 1)
-    relay(2)
-    scatter(0, 1)
-    grow_leave(0, 0)
-    grow_keep(0, 0)
-    scatter(2, 1)
-    mix(1)
-    grow_leave(2, 0)
-    grow_keep(2, 0)
-    pass_on(0, 0)
-    mix(0)
-    grow_leave(1, 1)
-    mix(2)
-    pass_on(2, 0)
-    grow_leave(0, 1)
-    grow_leave(2, 1)
+        if at == 1:
+            share_frames(1, 0)
+            scatter(1, 0, True)
+            scatter(1, 1, True)
 
     def unturn(origin, factor, put):
         def one(step, unused):
@@ -772,8 +782,6 @@
     def put_normed(column, rows, value):
         normed[column, rows, :] = value.astype(bf16)
 
-    unturn(work, scale, put_normed)
-
     def gather(picks, target):
         def one(step, unused):
             some = pl.ds(step * batch, batch)
@@ -783,33 +791,82 @@
 
         lax.fori_loop(0, terms // batch, one, 0)
 
+    def back_add():
+        for at in order:
+            first, (blocks, parts) = FIRSTS[at], PARTS[at]
+            for copy in scattered[at]:
+                copy.wait_recv()
+            for index in range(shares - 1):
+
+                def add(row, unused):
+                    arrived = back_in[at][index, row].astype(f32)
+                    for part in range(parts):
+                        back[first + part * blocks + row] += arrived[
+                            :, part * edges : (part + 1) * edges
+                        ]
+                    return unused
+
+                lax.fori_loop(0, blocks, add, 0)
+
+    share_frames(0, 0)
+    near_send(0)
+    back_leave(0, 0, 5)
+    relay(1)
+    forward(1, 0)
+    scatter(1, 0, False)
+    share_frames(2, 0)
+    share_frames(1, 1)
+    back_leave(2, 0, 3)
+    forward(1, 1)
+    share_frames(0, 1)
+    share_frames(2, 1)
+    scatter_both(0, 0)
+    near_send(2)
+    grow_leave(1, 0)
+    grow_keep(1, 0)
+    back_send(1, 2, 4)
+    back_send(0, 0, 5)
+    back_keep(1)
+    pass_on(1, 0)
+    pass_on(1, 1)
+    scatter_both(2, 0)
+    back_keep(0)
+    pass_on(1, 2)
+    pass_on(1, 3)
+    scatter(1, 1, False)
+    relay(0)
+    back_send(2, 0, 3)
+    grow_leave(0, 0)
+    grow_keep(0, 0)
+    scatter_both(0, 1)
+    scatter_both(2, 1)
+    back_keep(2)
+    mix(1)
+    grow_leave(1, 1)
+    grow_keep(1, 1)
+    pass_on(0, 0)
+    pass_on(0, 1)
+    relay(2)
+    grow_leave(2, 0)
+    grow_keep(2, 0)
+    mix(0)
+    mix(2)
+    unturn(work, scale, put_normed)
     gather(to_target, arrow)
     stored = [bring(arrow, update)]
-    for at in order:
-        grow_keep(at, 1)
-    for at in order:
-        first, (blocks, parts) = FIRSTS[at], PARTS[at]
-        for index, copy in enumerate(scattered[at]):
-            copy.wait_recv()
-
-            def add(row, unused):
-                arrived = back_in[at][index, row].astype(f32)
-                for part in range(parts):
-                    back[first + part * blocks + row] += arrived[
-                        :, part * edges : (part + 1) * edges
-                    ]
-                return unused
-
-            lax.fori_loop(0, blocks, add, 0)
+    back_add()
     unturn(back, None, put_normed)
-
     fold(to_halo, ends_out)
     ends = [
         links.start(ends_out.at[1], ends_in.at[0], after),
         links.start(ends_out.at[0], ends_in.at[1], before),
     ]
-
+    pass_on(2, 0)
     gather(to_source, work)
+    grow_leave(0, 1)
+    grow_keep(0, 1)
+    grow_leave(2, 1)
+    grow_keep(2, 1)
     for copy in ends:
         copy.wait_recv()
     unfold(ends_in, to_face)
@@ -903,7 +960,7 @@
     ]
     scratch += 4 * [((2, halo, terms * width), bf16)]
     scratch += 2 * [((8, atoms), f32), ((shares - 1, 8, atoms), f32)]
-    number = 11 * (shares - 1) + 15 + 30 + 12 + 4
+    number = 16 * (shares - 1) + 15 + 50 + 24 + 4
     anywhere = pl.BlockSpec(memory_space=pl.ANY)
     inside = pl.BlockSpec(memory_space=pltpu.VMEM)
     return pl.pallas_call(
@@ -920,11 +977,45 @@
         + [
             pltpu.SemaphoreType.DMA((number,)),
             pltpu.SemaphoreType.DMA((number,)),
-            pltpu.SemaphoreType.DMA((32,)),
+            pltpu.SemaphoreType.DMA((48,)),
         ],
         compiler_params=pltpu.CompilerParams(
             collective_id=0, has_side_effects=True, vmem_limit_bytes=67043328
         ),
+    )(*arrays)
+
+
+def carry_kernel(*refs):
+    count = (len(refs) - 1) // 3
+    sems = refs[-1]
+    origins, targets, held = refs[:count], refs[count : 2 * count], refs[2 * count : 3 * count]
+    reads = [
+        pltpu.make_async_copy(origin, here, sems.at[0, index])
+        for index, (origin, here) in enumerate(zip(origins, held))
+    ]
+    writes = [
+        pltpu.make_async_copy(here, target, sems.at[1, index])
+        for index, (here, target) in enumerate(zip(held, targets))
+    ]
+    for read in reads:
+        read.start()
+    for read, write in zip(reads, writes):
+        read.wait()
+        write.start()
+    for write in writes:
+        write.wait()
+
+
+def carry_out(arrays):
+    anywhere = [pl.BlockSpec(memory_space=pl.ANY)] * len(arrays)
+    return pl.pallas_call(
+        carry_kernel,
+        in_specs=anywhere,
+        out_specs=anywhere,
+        out_shape=[jax.ShapeDtypeStruct(array.shape, array.dtype) for array in arrays],
+        scratch_shapes=[pltpu.VMEM(array.shape, array.dtype) for array in arrays]
+        + [pltpu.SemaphoreType.DMA((2, len(arrays)))],
+        compiler_params=pltpu.CompilerParams(vmem_limit_bytes=67043328),
     )(*arrays)
 
 
@@ -1037,7 +1128,7 @@
         edge_weight[None, :],
     )
     sizes = (lax.axis_size("chan"), lax.axis_size("graph"))
-    update, grad_embed, done_zero, done_one, done_two = run_layer(arrays, sizes)
+    update, grad_embed, done_zero, done_one, done_two = carry_out(run_layer(arrays, sizes))
     grad_zero = jnp.transpose(done_zero, (0, 2, 1))
     grad_two = jnp.transpose(done_two, (0, 1, 3, 2))
     return (update, grad_embed, grad_zero, done_one, grad_two)

time: 129 us -> 110 us (0.85)
  the two profiles are of different devices: /device:TPU:25 before, /device:TPU:0 now
where the time goes in v2:
time: 110 us; the launch traced here: 109 us
  Pallas kernels  108 us (98%)
    pallas_call x1, Pallas kernels, run_layer(): pl.pallas_call(functools.partial(layer_kernel, shares, count), in_specs=[...  104 us
    pallas_call x1, Pallas kernels, carry_out(): pl.pallas_call(carry_kernel, in_specs=anywhere, out_specs=anywhere, out_s...  4.18 us

profile of v2, /device:TPU:0, one launch (start us, length us, event | category | flops | bytes accessed | tf_op | source)
XLA Modules:
  0.0 109.1 jit_solution(11984723735005910912)
XLA Ops:
  0.6 104.2 %shard_map.155 = (bf16[25,256,128]{2,1,0:T(8,128)(2,1)}, bf16[25,256,128]{2,1,0:T(8,128)(2,1)}, f32[5,160,256]{2,1,0:T(8,128)}, f32[2,4,256,128]{3,2,1,0:T(8,128)}, f32[2,3,96,256]{3,2,1,0:T(8,128)}) custom-call(bf16[25,256,128]{2,1,0:T(8,128)(2,1)} %refs_0_.1, bf16[25,256,128]{2,1,0:T(8,128)(2,1)} %refs_1_.1, f32[5,256]{1,0:T(8,128)} %refs_2_.1, ...), custom_call_target="tpu_custom_call" | custom-call | tf_op jit(solution)/shard_map/pallas_call | solution.py:966
  104.9 4.2 %shard_map.156 = (bf16[25,256,128]{2,1,0:T(8,128)(2,1)}, bf16[25,256,128]{2,1,0:T(8,128)(2,1)}, f32[5,160,256]{2,1,0:T(8,128)}, f32[2,4,256,128]{3,2,1,0:T(8,128)}, f32[2,3,96,256]{3,2,1,0:T(8,128)}) custom-call(bf16[25,256,128]{2,1,0:T(8,128)(2,1)} %get-tuple-element.15.refs_0_, bf16[25,256,128]{2,1,0:T(8,128)(2,1)} %get-tuple-element.16.refs_1_, ...), custom_call_target="tpu_custom_call" | custom-call | tf_op jit(solution)/shard_map/pallas_call | solution.py:1011

commit v3 on v2

--- a/solution.py
+++ b/solution.py
@@ -431,44 +431,6 @@
         for index, peer in enumerate(peers)
     ]
 
-    whole = own_squares
-    for index, copy in enumerate(summed):
-        copy.wait_recv()
-        whole = whole + square_in[index, :1, :]
-    inverse = lax.rsqrt(whole / (terms * channels) + EPSILON)
-    for degree in range(5):
-
-        def normal(term, unused):
-            normed[term] = (values[term].astype(f32) * inverse * gains[degree]).astype(bf16)
-            return unused
-
-        lax.fori_loop(degree * degree, (degree + 1) * (degree + 1), normal, 0)
-
-    def fold(picks, target):
-        def one(step, unused):
-            value = normed[pl.ds(step * batch, batch)].reshape(batch * width, atoms)
-            value = turned(picks, value).astype(bf16).reshape(2, halo, batch * width)
-            target[:, :, lanes(step * batch * width, batch * width)] = value
-            return unused
-
-        lax.fori_loop(0, terms // batch, one, 0)
-
-    def unfold(origin, picks):
-        def one(step, unused):
-            some = pl.ds(step * batch, batch)
-            value = origin[:, :, lanes(step * batch * width, batch * width)]
-            value = across(value.reshape(2 * halo, batch * width), picks)
-            work[some] += value.reshape(batch, width, atoms)
-            return unused
-
-        lax.fori_loop(0, terms // batch, one, 0)
-
-    fold(to_face, face_out)
-    halos = [
-        links.start(face_out.at[1], face_in.at[0], after),
-        links.start(face_out.at[0], face_in.at[1], before),
-    ]
-
     def spread(values_ref, picks):
         def one(step, unused):
             some = pl.ds(step * batch, batch)
@@ -520,15 +482,56 @@
             [links.start(spot, spot, flip(1)) for spot in spots],
         ]
 
-    for at in order:
-
+    def frame_grad(at):
         def put_grad(block, part, start, line):
             rows = pl.ds(pl.multiple_of(block * width + start, tall), tall)
             grads[at][rows, lanes((part * NEAR + slot) * edges, edges)] = (line * scale).astype(bf16)
 
         rotate(at, put_grad)
-        if at == 1:
-            near_send(1)
+
+    frame_grad(1)
+
+    whole = own_squares
+    for index, copy in enumerate(summed):
+        copy.wait_recv()
+        whole = whole + square_in[index, :1, :]
+    inverse = lax.rsqrt(whole / (terms * channels) + EPSILON)
+    for degree in range(5):
+
+        def normal(term, unused):
+            normed[term] = (values[term].astype(f32) * inverse * gains[degree]).astype(bf16)
+            return unused
+
+        lax.fori_loop(degree * degree, (degree + 1) * (degree + 1), normal, 0)
+
+    def fold(picks, target):
+        def one(step, unused):
+            value = normed[pl.ds(step * batch, batch)].reshape(batch * width, atoms)
+            value = turned(picks, value).astype(bf16).reshape(2, halo, batch * width)
+            target[:, :, lanes(step * batch * width, batch * width)] = value
+            return unused
+
+        lax.fori_loop(0, terms // batch, one, 0)
+
+    def unfold(origin, picks):
+        def one(step, unused):
+            some = pl.ds(step * batch, batch)
+            value = origin[:, :, lanes(step * batch * width, batch * width)]
+            value = across(value.reshape(2 * halo, batch * width), picks)
+            work[some] += value.reshape(batch, width, atoms)
+            return unused
+
+        lax.fori_loop(0, terms // batch, one, 0)
+
+    fold(to_face, face_out)
+    halos = [
+        links.start(face_out.at[1], face_in.at[0], after),
+        links.start(face_out.at[0], face_in.at[1], before),
+    ]
+
+    near_send(1)
+    frame_grad(0)
+    frame_grad(2)
     for at in (1, 2):
         blocks = PARTS[at][0]
         height = blocks * width
@@ -811,12 +814,12 @@
     share_frames(0, 0)
     near_send(0)
     back_leave(0, 0, 5)
+    back_leave(2, 0, 3)
     relay(1)
     forward(1, 0)
     scatter(1, 0, False)
     share_frames(2, 0)
     share_frames(1, 1)
-    back_leave(2, 0, 3)
     forward(1, 1)
     share_frames(0, 1)
     share_frames(2, 1)
@@ -826,10 +829,10 @@
     grow_keep(1, 0)
     back_send(1, 2, 4)
     back_send(0, 0, 5)
+    scatter_both(2, 0)
+    pass_on(1, 0)
     back_keep(1)
-    pass_on(1, 0)
     pass_on(1, 1)
-    scatter_both(2, 0)
     back_keep(0)
     pass_on(1, 2)
     pass_on(1, 3)
@@ -839,21 +842,21 @@
     grow_leave(0, 0)
     grow_keep(0, 0)
     scatter_both(0, 1)
+    back_keep(2)
     scatter_both(2, 1)
-    back_keep(2)
-    mix(1)
     grow_leave(1, 1)
     grow_keep(1, 1)
+    mix(1)
     pass_on(0, 0)
     pass_on(0, 1)
+    mix(0)
     relay(2)
-    grow_leave(2, 0)
-    grow_keep(2, 0)
-    mix(0)
     mix(2)
     unturn(work, scale, put_normed)
     gather(to_target, arrow)
     stored = [bring(arrow, update)]
+    grow_leave(2, 0)
+    grow_keep(2, 0)
     back_add()
     unturn(back, None, put_normed)
     fold(to_halo, ends_out)
@@ -861,11 +864,11 @@
         links.start(ends_out.at[1], ends_in.at[0], after),
         links.start(ends_out.at[0], ends_in.at[1], before),
     ]
+    grow_leave(0, 1)
     pass_on(2, 0)
+    grow_leave(2, 1)
     gather(to_source, work)
-    grow_leave(0, 1)
     grow_keep(0, 1)
-    grow_leave(2, 1)
     grow_keep(2, 1)
     for copy in ends:
         copy.wait_recv()

time: 110 us -> 108 us (0.982)
    pallas_call x1, Pallas kernels: 104 us -> 103 us  [run_layer(): pl.pallas_call(functools.partial(layer_kernel, shares, count), in_specs=[...]
where the time goes in v3:
time: 108 us
  Pallas kernels  107 us (99%)
    pallas_call x1, Pallas kernels, run_layer(): pl.pallas_call(functools.partial(layer_kernel, shares, count), in_specs=[...  103 us
    pallas_call x1, Pallas kernels, carry_out(): pl.pallas_call(carry_kernel, in_specs=anywhere, out_specs=anywhere, out_s...  4.18 us

profile of v3, /device:TPU:0, one launch (start us, length us, event | category | flops | bytes accessed | tf_op | source)
XLA Modules:
  0.0 107.6 jit_solution(4323787694439211185)
XLA Ops:
  0.6 102.8 %shard_map.155 = (bf16[25,256,128]{2,1,0:T(8,128)(2,1)}, bf16[25,256,128]{2,1,0:T(8,128)(2,1)}, f32[5,160,256]{2,1,0:T(8,128)}, f32[2,4,256,128]{3,2,1,0:T(8,128)}, f32[2,3,96,256]{3,2,1,0:T(8,128)}) custom-call(bf16[25,256,128]{2,1,0:T(8,128)(2,1)} %refs_0_.1, bf16[25,256,128]{2,1,0:T(8,128)(2,1)} %refs_1_.1, f32[5,256]{1,0:T(8,128)} %refs_2_.1, ...), custom_call_target="tpu_custom_call" | custom-call | tf_op jit(solution)/shard_map/pallas_call | solution.py:969
  103.4 4.2 %shard_map.156 = (bf16[25,256,128]{2,1,0:T(8,128)(2,1)}, bf16[25,256,128]{2,1,0:T(8,128)(2,1)}, f32[5,160,256]{2,1,0:T(8,128)}, f32[2,4,256,128]{3,2,1,0:T(8,128)}, f32[2,3,96,256]{3,2,1,0:T(8,128)}) custom-call(bf16[25,256,128]{2,1,0:T(8,128)(2,1)} %get-tuple-element.15.refs_0_, bf16[25,256,128]{2,1,0:T(8,128)(2,1)} %get-tuple-element.16.refs_1_, ...), custom_call_target="tpu_custom_call" | custom-call | tf_op jit(solution)/shard_map/pallas_call | solution.py:1014

commit v4 on v3

--- a/solution.py
+++ b/solution.py
@@ -328,7 +328,7 @@
 
 
 def layer_kernel(shares, count, *refs):
-    (embed, cotangent, gain, w_zero, w_one, w_two, table) = refs[:7]
+    (embed, cotangent, gain, w_zero, w_one, w_two, table_home) = refs[:7]
     (face_row, source_row, target_row, which_row, weight_row) = refs[7:12]
     (update, grad_embed, out_zero, out_one, out_two) = refs[12:17]
     weights = refs[17:20]
@@ -341,7 +341,8 @@
     (work, back, arrow, values, normed, rot, gains) = refs[49:56]
     (face_out, face_in, ends_out, ends_in) = refs[56:60]
     (square_out, square_in, tally_out, tally_in) = refs[60:64]
-    sends, recvs, local_sems = refs[64:67]
+    table = refs[64]
+    sends, recvs, local_sems = refs[65:68]
     outs = (out_zero, out_one, out_two)
     f32, bf16 = jnp.float32, jnp.bfloat16
     terms, width, atoms = values.shape
@@ -372,6 +373,7 @@
         copies.append(copy)
         return copy
 
+    load_table = bring(table_home, table)
     load_embed = bring(embed, values)
     load_cotangent = bring(cotangent, arrow)
     order = (1, 0, 2)
@@ -386,6 +388,7 @@
         )
     links = Links(sends, recvs)
     which = hot(table.shape[2], which_row[...])
+    load_table.wait()
 
     def turn(term, unused):
         rest, total = table[term], None
@@ -963,12 +966,13 @@
     ]
     scratch += 4 * [((2, halo, terms * width), bf16)]
     scratch += 2 * [((8, atoms), f32), ((shares - 1, 8, atoms), f32)]
+    scratch += [(arrays[6].shape, f32)]
     number = 16 * (shares - 1) + 15 + 50 + 24 + 4
     anywhere = pl.BlockSpec(memory_space=pl.ANY)
     inside = pl.BlockSpec(memory_space=pltpu.VMEM)
     return pl.pallas_call(
         functools.partial(layer_kernel, shares, count),
-        in_specs=[anywhere] * 2 + [inside] + [anywhere] * 3 + [inside] * 6,
+        in_specs=[anywhere] * 2 + [inside] + [anywhere] * 4 + [inside] * 5,
         out_specs=[anywhere] * 5,
         out_shape=[jax.ShapeDtypeStruct(embed.shape, bf16)] * 2
         + [

time: 108 us -> 108 us (level)
  no operation moved by 1% of the time
where the time goes in v4:
time: 108 us
  Pallas kernels  108 us (100%)
    pallas_call x1, Pallas kernels, run_layer(): pl.pallas_call(functools.partial(layer_kernel, shares, count), in_specs=[...  103 us
    pallas_call x1, Pallas kernels, carry_out(): pl.pallas_call(carry_kernel, in_specs=anywhere, out_specs=anywhere, out_s...  4.18 us

profile of v4, /device:TPU:0, one launch (start us, length us, event | category | flops | bytes accessed | tf_op | source)
XLA Modules:
  0.0 108.3 jit_solution(15243936525588461724)
XLA Ops:
  0.6 103.5 %shard_map.155 = (bf16[25,256,128]{2,1,0:T(8,128)(2,1)}, bf16[25,256,128]{2,1,0:T(8,128)(2,1)}, f32[5,160,256]{2,1,0:T(8,128)}, f32[2,4,256,128]{3,2,1,0:T(8,128)}, f32[2,3,96,256]{3,2,1,0:T(8,128)}) custom-call(bf16[25,256,128]{2,1,0:T(8,128)(2,1)} %refs_0_.1, bf16[25,256,128]{2,1,0:T(8,128)(2,1)} %refs_1_.1, f32[5,256]{1,0:T(8,128)} %refs_2_.1, ...), custom_call_target="tpu_custom_call" | custom-call | tf_op jit(solution)/shard_map/pallas_call | solution.py:973
  104.1 4.2 %shard_map.156 = (bf16[25,256,128]{2,1,0:T(8,128)(2,1)}, bf16[25,256,128]{2,1,0:T(8,128)(2,1)}, f32[5,160,256]{2,1,0:T(8,128)}, f32[2,4,256,128]{3,2,1,0:T(8,128)}, f32[2,3,96,256]{3,2,1,0:T(8,128)}) custom-call(bf16[25,256,128]{2,1,0:T(8,128)(2,1)} %get-tuple-element.15.refs_0_, bf16[25,256,128]{2,1,0:T(8,128)(2,1)} %get-tuple-element.16.refs_1_, ...), custom_call_target="tpu_custom_call" | custom-call | tf_op jit(solution)/shard_map/pallas_call | solution.py:1018
